TPU v7x, 32 devices: a whole 2x2x4 slice. The times are simulated.
32 devices in a mesh: outer: 4 (over y, core), inner: 8 (over z, x).
Axes of the slice: x: 2, y: 2, z: 4, core: 2. Of those that a mesh axis runs over, the one named last changes fastest.
Arguments:
- query_rows: bfloat16 [8192, 1024], P(('outer', 'inner')), may hold values from -6 to 6
- key_rows: bfloat16 [8192, 1024], P(('outer', 'inner')), may hold values from -6 to 6
- value_rows: bfloat16 [8192, 1024], P(('outer', 'inner')), may hold values from -6 to 6
- log_decay: float32 [8, 8192], P(None, ('outer', 'inner')), may hold values from -0.8 to 0, as said below
- grad_out: bfloat16 [8192, 1024], P(('outer', 'inner')), may hold values from -6 to 6
Outputs:
- attended: bfloat16 [8192, 1024], P(('outer', 'inner'))
- grad_queries: bfloat16 [8192, 1024], P(('outer', 'inner'))
- grad_keys: bfloat16 [8192, 1024], P(('outer', 'inner'))
- grad_values: bfloat16 [8192, 1024], P(('outer', 'inner'))
Inputs may be any that keep to these rules, and one draw needn't show every extreme that they name: `log_decay`: every entry is negative.
All inputs are finite; a program needn't handle non-finite values.
Results may differ from a plain program's by a relative error of at most 0.0063.
Values sent between devices are 32-bit elements; how exact they have to be, the bound alone decides.
A program may use at most 320 MiB of HBM per device.

v0:
```python
import math

import jax
import jax.numpy as jnp
from jax import lax
from jax.sharding import PartitionSpec as P

EPSILON = 1e-06


def entering_2(array, axis, combine, identity, reverse):
    size, place = (lax.axis_size(axis), lax.axis_index(axis))
    everything = jax.tree.map(lambda part: lax.all_gather(part, axis), array)
    start = jax.tree.map(
        lambda part, zero: jnp.broadcast_to(jnp.asarray(zero, part.dtype), part.shape),
        array,
        identity,
    )

    def turn(k, before):
        at = size - 1 - k if reverse else k
        reached = at > place if reverse else at < place
        new = combine(before, jax.tree.map(lambda part: part[at], everything))
        return jax.tree.map(lambda a, b: jnp.where(reached, a, b), new, before)

    return lax.fori_loop(0, size, turn, start)


def combine(earlier, latter):
    return (earlier[0] + latter[0], jnp.exp(latter[0])[:, None, None] * earlier[1] + latter[1])


def carried(states, backward):
    identity = (jnp.zeros_like(states[0]), jnp.zeros_like(states[1]))
    return entering_2(states, ("outer", "inner"), combine, identity, backward)


def causal_decay(running):
    length_rows = running.shape[1]
    row_index = lax.broadcasted_iota(jnp.int32, (length_rows, length_rows), 0)
    col_index = lax.broadcasted_iota(jnp.int32, (length_rows, length_rows), 1)
    causal = (col_index <= row_index)[None]
    gaps = running[:, :, None] - running[:, None, :]
    return jnp.where(causal, jnp.exp(jnp.where(causal, gaps, 0.0)), 0.0)


def body(query_rows, key_rows, value_rows, log_decay, grad_out):
    head_count = log_decay.shape[0]
    length_rows = log_decay.shape[1]
    head_size = query_rows.shape[1] // head_count
    scaling = 1.0 / math.sqrt(head_size)
    block_shape = (length_rows, head_count, head_size)
    queries = query_rows.reshape(block_shape)
    keys_local = key_rows.reshape(block_shape)
    values = value_rows.reshape(block_shape)
    running = jnp.cumsum(log_decay, axis=1)
    totals = running[:, -1]
    growth = jnp.exp(running).T[:, :, None]
    shrink = jnp.exp(totals[:, None] - running).T[:, :, None]
    query_dec = (queries.astype(jnp.float32) * growth).astype(jnp.bfloat16)
    key_dec = (keys_local.astype(jnp.float32) * shrink).astype(jnp.bfloat16)
    block_state = jnp.einsum("the,thf->hef", key_dec, values, preferred_element_type=jnp.float32)
    _, entering = carried((totals, block_state), False)
    decay_mat = causal_decay(running)
    scores = jnp.einsum("the,she->hts", queries, keys_local, preferred_element_type=jnp.float32)
    weights = (scores * scaling * decay_mat).astype(jnp.bfloat16)
    entering_half = entering.astype(jnp.bfloat16)
    mixed = jnp.einsum("hts,shf->thf", weights, values, preferred_element_type=jnp.float32)
    mixed = mixed + scaling * jnp.einsum(
        "the,hef->thf", query_dec, entering_half, preferred_element_type=jnp.float32
    )
    inverse = lax.rsqrt(jnp.mean(mixed * mixed, axis=2, keepdims=True) + EPSILON)
    normed = mixed * inverse
    grad_normed = grad_out.reshape(block_shape).astype(jnp.float32)
    grad_mixed = (
        inverse * (grad_normed - normed * jnp.mean(grad_normed * normed, axis=2, keepdims=True))
    ).astype(jnp.bfloat16)
    back_state = scaling * jnp.einsum(
        "the,thf->hef", query_dec, grad_mixed, preferred_element_type=jnp.float32
    )
    _, leaving = carried((totals, back_state), True)
    grad_prob = jnp.einsum("thf,shf->hts", grad_mixed, values, preferred_element_type=jnp.float32)
    grad_score = (grad_prob * scaling * decay_mat).astype(jnp.bfloat16)
    grad_q = jnp.einsum("hts,she->the", grad_score, keys_local, preferred_element_type=jnp.float32)
    grad_q = grad_q + scaling * growth * jnp.einsum(
        "thf,hef->the", grad_mixed, entering_half, preferred_element_type=jnp.float32
    )
    grad_v = jnp.einsum("hts,thf->shf", weights, grad_mixed, preferred_element_type=jnp.float32)
    grad_k = jnp.einsum("hts,the->she", grad_score, queries, preferred_element_type=jnp.float32)
    leaving_half = leaving.astype(jnp.bfloat16)
    grad_k = grad_k + shrink * jnp.einsum(
        "shf,hef->she", values, leaving_half, preferred_element_type=jnp.float32
    )
    grad_v = grad_v + jnp.einsum(
        "she,hef->shf", key_dec, leaving_half, preferred_element_type=jnp.float32
    )
    attended = normed.astype(jnp.bfloat16).reshape(length_rows, -1)
    return (
        attended,
        grad_q.astype(jnp.bfloat16).reshape(length_rows, -1),
        grad_k.astype(jnp.bfloat16).reshape(length_rows, -1),
        grad_v.astype(jnp.bfloat16).reshape(length_rows, -1),
    )


def solution(mesh):
    return jax.shard_map(
        body,
        mesh=mesh,
        in_specs=(
            P(("outer", "inner"), None),
            P(("outer", "inner"), None),
            P(("outer", "inner"), None),
            P(None, ("outer", "inner")),
            P(("outer", "inner"), None),
        ),
        out_specs=(
            P(("outer", "inner"), None),
            P(("outer", "inner"), None),
            P(("outer", "inner"), None),
            P(("outer", "inner"), None),
        ),
        check_vma=False,
    )
```

profile of v0, /device:TPU:0, one launch (start us, length us, event | category | flops | bytes accessed | tf_op | source)
XLA Modules:
  0.0 335.5 jit_solution(9522661758703197729)
XLA Ops:
  7.2 1.3 reduce-window.6
  9.1 1.3 copy.77
  11.8 43.3 %all-reduce = f32[256]{0:T(256)S(1)} all-reduce(f32[256]{0:T(256)S(1)} %dynamic-update-slice), channel_id=2, replica_groups=mesh['outer'=4,'inner'=8] {'outer','inner'}, use_global_device_ids=true, to_apply=%add | all-reduce | flops 256 | bytes 2048
  55.5 1.4 copy.85
  58.8 1.5 convolution_bitcast_fusion.4
  60.3 69.6 %all-gather.6.cloned.1.call-done = f32[256,128,128]{2,1,0:T(8,128)} async-done(((f32[8,128,128]{2,1,0:T(8,128)}), f32[256,128,128]{2,1,0:T(8,128)}) %all-gather.6.cloned.1.call-update) | async-done | bytes 16777232 | tf_op jit(solution)/shard_map/all_gather | solution.py:13
  129.9 39.0 %while.30 = (s32[]{:T(128)}, f32[8,128,128]{2,1,0:T(8,128)S(1)}, s32[]{:T(128)}, f32[32,8]{1,0:T(8,128)S(1)}, f32[32,8,128,128]{3,2,1,0:T(8,128)}, /*index=5*/s32[]{:T(128)}, s32[]{:T(128)}) while((s32[]{:T(128)}, f32[8,128,128]{2,1,0:T(8,128)S(1)}, s32[]{:T(128)}, f32[32,8]{1,0:T(8,128)S(1)}, f32[32,8,128,128]{3,2,1,0:T(8,128)}, ...), condition=%wide.region_3.4_spmd.clone, body=%wide.region_2.3_spmd.clone.sunk | while | flops 524292 | bytes 1573073 | solution.py:26
  131.1 1.2 fusion.43
  132.3 1.2 fusion.43
  133.5 1.2 fusion.43
  134.8 1.2 fusion.43
  136.0 1.2 fusion.43
  137.2 1.2 fusion.43
  138.4 1.2 fusion.43
  139.6 1.2 fusion.43
  140.9 1.2 fusion.43
  142.1 1.2 fusion.43
  143.3 1.2 fusion.43
  144.5 1.2 fusion.43
  148.2 1.2 fusion.43
  149.4 1.2 fusion.43
  151.8 1.2 fusion.43
  153.1 1.2 fusion.43
  155.5 1.2 fusion.43
  156.7 1.2 fusion.43
  160.4 1.2 fusion.43
  164.0 1.2 fusion.43
  167.7 1.2 fusion.43
  168.9 1.6 multiply_reduce_fusion.1
  176.7 2.6 fusion.24
  179.7 105.9 %all-gather.8.cloned.1.call-done = f32[256,128,128]{2,1,0:T(8,128)} async-done(((f32[8,128,128]{2,1,0:T(8,128)}), f32[256,128,128]{2,1,0:T(8,128)}) %all-gather.8.cloned.1.call-update) | async-done | bytes 16777232 | tf_op jit(solution)/shard_map/all_gather | solution.py:13
  285.6 39.2 %while.31 = (s32[]{:T(128)}, f32[8,128,128]{2,1,0:T(8,128)S(1)}, s32[]{:T(128)}, f32[32,8]{1,0:T(8,128)S(1)}, f32[32,8,128,128]{3,2,1,0:T(8,128)}, /*index=5*/s32[]{:T(128)}, s32[]{:T(128)}, s32[]{:T(128)}, s32[]{:T(128)}) while((s32[]{:T(128)}, f32[8,128,128]{2,1,0:T(8,128)S(1)}, s32[]{:T(128)}, f32[32,8]{1,0:T(8,128)S(1)}, ...), condition=%wide.region_7.8_spmd.clone, body=%wide.region_6.7_spmd.clone.sunk | while | flops 524296 | bytes 1573135 | solution.py:26
  289.3 1.2 fusion.44
  290.5 1.2 fusion.44
  291.7 1.2 fusion.44
  296.6 1.2 fusion.44
  297.9 1.2 fusion.44
  299.1 1.2 fusion.44
  304.0 1.2 fusion.44
  305.2 1.2 fusion.44
  306.4 1.2 fusion.44
  312.6 1.2 fusion.44
  313.8 1.2 fusion.44
  315.0 1.2 fusion.44
  319.9 1.2 fusion.44
  321.1 1.2 fusion.44
  322.4 1.2 fusion.44
  324.8 1.6 fusion.10
  (143 shorter events, 46.6 us)
Async XLA Ops:
  7.2 3.2 copy-start
  7.2 48.1 %copy-start.8 = (bf16[256,1024]{1,0:T(8,128)(2,1)S(1)}, bf16[256,1024]{1,0:T(8,128)(2,1)}, u32[]{:S(2)}) copy-start(bf16[256,1024]{1,0:T(8,128)(2,1)} %param.9) | copy-start | bytes 1572868
  7.2 122.7 %all-gather.6.cloned.1.call-start = ((), (), s32[]{:S(2)}) async-start(), calls=%async_computation | async-start | bytes 17301504 | tf_op jit(solution)/shard_map/all_gather | solution.py:13
  11.5 274.1 %all-gather.8.cloned.1.call-start = ((), (), s32[]{:S(2)}) async-start(), calls=%async_computation.1 | async-start | bytes 17301504 | tf_op jit(solution)/shard_map/all_gather | solution.py:13
  55.5 113.4 %copy-start.1 = (bf16[256,1024]{0,1:T(8,128)(2,1)}, bf16[256,1024]{0,1:T(8,128)(2,1)S(1)}, u32[]{:S(2)}) copy-start(bf16[256,1024]{0,1:T(8,128)(2,1)S(1)} %copy.106) | copy-start | bytes 1572868
  57.8 1.0 copy-start.4
  170.7 1.1 copy-start.2
  171.7 1.2 copy-start.7
  174.7 1.0 copy-start.5
  175.7 3.6 %copy-start.3 = (bf16[256,1024]{0,1:T(8,128)(2,1)S(1)}, bf16[256,1024]{0,1:T(8,128)(2,1)}, u32[]{:S(2)}) copy-start(bf16[256,1024]{0,1:T(8,128)(2,1)} %copy-done.1) | copy-start | bytes 1572868
  176.7 2.6 copy-start.6
Sparse Core Ops, SparseCore 0:
  11.6 118.2 all-gather.5
  173.0 112.5 all-gather.7
where the time goes:
time: 339 us; the launch traced here: 336 us
  waiting for transfers between devices  176 us (52%)
  other arithmetic  78 us (23%)
  blocking collectives  43.3 us (13%)
  between operations  14.3 us (4%)
  matrix products  12.5 us (4%)
  local copies, waits for them, and re-layouts  9.61 us (3%)
    all_gather x2, waiting for transfers between devices, entering_2(): everything = jax.tree.map(lambda part: lax.all_gather(part, axis), array)  176 us
    select_n x64, other arithmetic, turn(): return jax.tree.map(lambda a, b: jnp.where(reached, a, b), new, before)  75.2 us
    unnamed x1, blocking collectives  43.3 us
    unnamed x25, local copies, waits for them, and re-layouts  6.79 us
  transfers between devices with their start and end apart: 2, of which 2 were waited for; matrix products, arithmetic and copies ran while one was open for 3% of the time, Pallas kernels for 0%

commit v1 on v0

v1 whole, which is shorter than its diff:
```python
import functools
import math

import jax
import jax.numpy as jnp
from jax import lax
from jax.experimental import pallas as pl
from jax.experimental.pallas import tpu as pltpu
from jax.sharding import PartitionSpec as P

EPSILON = 1e-06
F32 = jnp.float32
BF16 = jnp.bfloat16
MESH = pl.DeviceIdType.MESH


def dot(a, b, da, db):
    return lax.dot_general(a, b, (((da,), (db,)), ((), ())), preferred_element_type=F32)


def kernel(outer_size, inner_size, q_ref, k_ref, v_ref, decay_ref, g_ref,
           att_ref, gq_ref, gk_ref, gv_ref,
           run_ref, col_ref, tot_ref, fac_ref, facs_ref, dec_ref, w_ref, kd_ref, mix_ref, gm_ref,
           send1, recv1, out1, ret1, send2, recv2, out2, ret2, ent_ref, gkl_ref, gvl_ref,
           send_sems, recv_sems):
    n = outer_size * inner_size
    heads, tokens = decay_ref.shape
    size = q_ref.shape[1] // heads
    scaling = 1.0 / math.sqrt(size)
    per_head = n // heads
    rows = size // per_head
    place_o, place_i = lax.axis_index("outer"), lax.axis_index("inner")
    me = place_o * inner_size + place_i

    def partner(i):
        t = i // outer_size
        step_o = (i % outer_size + 1) % outer_size
        step_i = inner_size // 2 + ((t + 1) // 2) * (2 * (t % 2) - 1) + inner_size
        return (place_o + step_o) % outer_size, (place_i + step_i) % inner_size

    def each_partner(act):
        def turn(i, carry):
            act(*partner(i))
            return carry
        lax.fori_loop(0, n - 1, turn, 0)

    def exchange(source_of, target, phase):
        def act(o, i):
            pltpu.make_async_remote_copy(
                src_ref=source_of(o * inner_size + i), dst_ref=target.at[me],
                send_sem=send_sems.at[phase], recv_sem=recv_sems.at[phase],
                device_id=(o, i), device_id_type=MESH).start()
        each_partner(act)

    def drain(buffer, sem):
        part = buffer.at[pl.ds(0, n - 1)]
        pltpu.make_async_copy(part, part, sem).wait()

    def each_head(act):
        def turn(i, carry):
            act(2 * i)
            act(2 * i + 1)
            return carry
        lax.fori_loop(0, heads // 2, turn, 0)

    def span(h):
        return pl.ds(pl.multiple_of(h * size, size), size)

    def put_state(target, h, state):
        if rows % 8 == 0:
            target[pl.ds(h * per_head, per_head)] = state.reshape(per_head, rows, size)
        else:
            for p in range(per_head):
                target[h * per_head + p] = state[p * rows:(p + 1) * rows]

    def get_state(source, h):
        if rows % 8 == 0:
            return source[pl.ds(h * per_head, per_head)].reshape(size, size)
        return jnp.concatenate([source[h * per_head + p] for p in range(per_head)], axis=0)

    barrier = pltpu.get_barrier_semaphore()
    each_partner(lambda o, i: pl.semaphore_signal(barrier, inc=1, device_id=(o, i), device_id_type=MESH))

    running = decay_ref[...]
    lane = lax.broadcasted_iota(jnp.int32, (heads, tokens), 1)
    shift = 1
    while shift < tokens:
        running = running + jnp.where(lane >= shift, pltpu.roll(running, shift, 1), 0.0)
        shift *= 2
    run_ref[...] = running
    for h in range(heads):
        row = running[h:h + 1]
        col_ref[h] = jnp.broadcast_to(row, (size, tokens)).T
        total = jnp.broadcast_to(row[:, tokens - 1:], (1, size))
        tot_ref[h] = total
        fac_ref[h] = jnp.exp(total)

    def state_of(h):
        cols = span(h)
        shrink = jnp.exp(tot_ref[h] - col_ref[h])
        key_dec = (k_ref[:, cols].astype(F32) * shrink).astype(BF16)
        kd_ref[:, cols] = key_dec
        put_state(send1, h, dot(key_dec, v_ref[:, cols], 0, 0))

    each_head(state_of)
    pl.semaphore_wait(barrier, n - 1)
    exchange(lambda c: fac_ref.at[c // per_head], facs_ref, 4)
    exchange(lambda c: send1.at[c], recv1, 0)
    facs_ref[me] = fac_ref[me // per_head]
    recv1[me] = send1[me]

    t_index = lax.broadcasted_iota(jnp.int32, (tokens, tokens), 0)
    s_index = lax.broadcasted_iota(jnp.int32, (tokens, tokens), 1)
    causal = s_index <= t_index

    def local_mix(h):
        cols = span(h)
        column = jnp.concatenate([col_ref[h]] * (tokens // size), axis=1)
        gaps = column - run_ref[pl.ds(h, 1)]
        decay = jnp.where(causal, jnp.exp(jnp.where(causal, gaps, 0.0)), 0.0) * scaling
        dec_ref[h] = decay
        weights = (dot(q_ref[:, cols], k_ref[:, cols], 1, 1) * decay).astype(BF16)
        w_ref[h] = weights
        mix_ref[:, cols] = dot(weights, v_ref[:, cols], 1, 0)

    each_head(local_mix)

    def scan(source, target, backward):
        def turn(i, state):
            at = n - 1 - i if backward else i
            target[at] = state
            return facs_ref[at] * state + source[at]
        lax.fori_loop(0, n, turn, jnp.zeros((rows, size), F32))

    drain(facs_ref, recv_sems.at[4])
    drain(recv1, recv_sems.at[0])
    scan(recv1, out1, False)
    exchange(lambda c: out1.at[c], ret1, 1)
    ret1[me] = out1[me]
    drain(ret1, recv_sems.at[1])

    def mix(h):
        cols = span(h)
        entering = get_state(ret1, h).astype(BF16)
        ent_ref[h] = entering
        growth = jnp.exp(col_ref[h])
        query_dec = (q_ref[:, cols].astype(F32) * growth).astype(BF16)
        mixed = mix_ref[:, cols] + scaling * dot(query_dec, entering, 1, 0)
        inverse = lax.rsqrt(jnp.mean(mixed * mixed, axis=1, keepdims=True) + EPSILON)
        normed = mixed * inverse
        att_ref[:, cols] = normed.astype(BF16)
        g = g_ref[:, cols].astype(F32)
        grad_mixed = (inverse * (g - normed * jnp.mean(g * normed, axis=1, keepdims=True))).astype(BF16)
        gm_ref[:, cols] = grad_mixed
        put_state(send2, h, scaling * dot(query_dec, grad_mixed, 0, 0))

    each_head(mix)
    exchange(lambda c: send2.at[c], recv2, 2)
    recv2[me] = send2[me]

    def local_grads(h):
        cols = span(h)
        grad_mixed = gm_ref[:, cols]
        grad_score = (dot(grad_mixed, v_ref[:, cols], 1, 1) * dec_ref[h]).astype(BF16)
        far = (scaling * jnp.exp(col_ref[h])) * dot(grad_mixed, ent_ref[h], 1, 1)
        gq_ref[:, cols] = (dot(grad_score, k_ref[:, cols], 1, 0) + far).astype(BF16)
        gkl_ref[:, cols] = dot(grad_score, q_ref[:, cols], 0, 0)
        gvl_ref[:, cols] = dot(w_ref[h], grad_mixed, 0, 0)

    each_head(local_grads)
    drain(recv2, recv_sems.at[2])
    scan(recv2, out2, True)
    exchange(lambda c: out2.at[c], ret2, 3)
    ret2[me] = out2[me]
    drain(ret2, recv_sems.at[3])

    def far_grads(h):
        cols = span(h)
        leaving = get_state(ret2, h).astype(BF16)
        shrink = jnp.exp(tot_ref[h] - col_ref[h])
        gk_ref[:, cols] = (gkl_ref[:, cols] + shrink * dot(v_ref[:, cols], leaving, 1, 1)).astype(BF16)
        gv_ref[:, cols] = (gvl_ref[:, cols] + dot(kd_ref[:, cols], leaving, 1, 0)).astype(BF16)

    each_head(far_grads)
    drain(facs_ref, send_sems.at[4])
    for phase, buffer in enumerate((send1, out1, send2, out2)):
        drain(buffer, send_sems.at[phase])


def body(outer_size, inner_size, query_rows, key_rows, value_rows, log_decay, grad_out):
    n = outer_size * inner_size
    heads, tokens = log_decay.shape
    wide = query_rows.shape[1]
    size = wide // heads
    rows = heads * size // n
    pieces = pltpu.VMEM((n, rows, size), F32)
    vmem = pl.BlockSpec(memory_space=pltpu.VMEM)
    return pl.pallas_call(
        functools.partial(kernel, outer_size, inner_size),
        out_shape=[jax.ShapeDtypeStruct((tokens, wide), BF16)] * 4,
        in_specs=[vmem] * 5,
        out_specs=[vmem] * 4,
        scratch_shapes=[
            pltpu.VMEM((heads, tokens), F32),
            pltpu.VMEM((heads, tokens, size), F32),
            pltpu.VMEM((heads, 1, size), F32),
            pltpu.VMEM((heads, 1, size), F32),
            pltpu.VMEM((n, 1, size), F32),
            pltpu.VMEM((heads, tokens, tokens), F32),
            pltpu.VMEM((heads, tokens, tokens), BF16),
            pltpu.VMEM((tokens, wide), BF16),
            pltpu.VMEM((tokens, wide), F32),
            pltpu.VMEM((tokens, wide), BF16),
            pieces, pieces, pieces, pieces, pieces, pieces, pieces, pieces,
            pltpu.VMEM((heads, size, size), BF16),
            pltpu.VMEM((tokens, wide), F32),
            pltpu.VMEM((tokens, wide), F32),
            pltpu.SemaphoreType.DMA((5,)),
            pltpu.SemaphoreType.DMA((5,)),
        ],
        compiler_params=pltpu.CompilerParams(
            collective_id=0, has_side_effects=True, vmem_limit_bytes=48 * 1024 * 1024),
    )(query_rows, key_rows, value_rows, log_decay, grad_out)


def solution(mesh):
    both = ("outer", "inner")
    row_spec = P(both, None)
    return jax.shard_map(
        functools.partial(body, mesh.shape["outer"], mesh.shape["inner"]),
        mesh=mesh,
        in_specs=(row_spec, row_spec, row_spec, P(None, both), row_spec),
        out_specs=(row_spec,) * 4,
        check_vma=False,
    )
```

time: 339 us -> 69.1 us (0.20)
  waiting for transfers between devices: 176 us -> 0 us
  other arithmetic: 78 us -> 0 us
  Pallas kernels: 0 us -> 60 us
  blocking collectives: 43.3 us -> 0 us
  between operations: 14.3 us -> 0.65 us
  matrix products: 12.5 us -> 0 us
    all_gather x2 -> x0, waiting for transfers between devices: 176 us -> none  [entering_2(): everything = jax.tree.map(lambda part: lax.all_gather(part, axis), array)]
    select_n x64 -> x0, other arithmetic: 75.2 us -> none  [turn(): return jax.tree.map(lambda a, b: jnp.where(reached, a, b), new, before)]
    pallas_call x0 -> x1, Pallas kernels: none -> 60 us  [body(): pl.pallas_call(functools.partial(kernel, outer_size, inner_size), out_sha...]
    unnamed x1 -> x0, blocking collectives: 43.3 us -> none
    dot_general x12 -> x0, matrix products: 12.5 us -> none  [the longest x1 2.62 us: body(): jnp.einsum('hts,thf->shf', weights, grad_mixed, preferred_element_type=jn...]
    unnamed x25 -> x14, local copies, waits for them, and re-layouts: 6.79 us -> 8.03 us
  transfers between devices with their start and end apart: 2 -> 0, of which waited for: 2 -> 0; matrix products, arithmetic and copies ran while one was open for 3% -> 0% of each run, Pallas kernels for 0% -> 0%
where the time goes in v1:
time: 69.1 us; the launch traced here: 68.7 us
  Pallas kernels  60 us (87%)
  local copies, waits for them, and re-layouts  8.03 us (12%)
    pallas_call x1, Pallas kernels, body(): pl.pallas_call(functools.partial(kernel, outer_size, inner_size), out_sha...  60 us
    unnamed x14, local copies, waits for them, and re-layouts  8.03 us

profile of v1, /device:TPU:0, one launch (start us, length us, event | category | flops | bytes accessed | tf_op | source)
XLA Modules:
  0.0 68.7 jit_solution(2119441249008125546)
XLA Ops:
  0.6 0.0 copy-start
  0.6 1.0 %copy-done = bf16[256,1024]{1,0:T(8,128)(2,1)S(1)} copy-done((bf16[256,1024]{1,0:T(8,128)(2,1)S(1)}, bf16[256,1024]{1,0:T(8,128)(2,1)}, u32[]{:S(2)}) %copy-start) | copy-done | bytes 524312
  1.7 0.0 copy-start.1
  1.7 1.0 %copy-done.1 = bf16[256,1024]{1,0:T(8,128)(2,1)S(1)} copy-done((bf16[256,1024]{1,0:T(8,128)(2,1)S(1)}, bf16[256,1024]{1,0:T(8,128)(2,1)}, u32[]{:S(2)}) %copy-start.1) | copy-done | bytes 524312
  2.7 0.0 copy-start.2
  2.7 1.0 %copy-done.2 = bf16[256,1024]{1,0:T(8,128)(2,1)S(1)} copy-done((bf16[256,1024]{1,0:T(8,128)(2,1)S(1)}, bf16[256,1024]{1,0:T(8,128)(2,1)}, u32[]{:S(2)}) %copy-start.2) | copy-done | bytes 524312
  3.8 0.0 copy-start.3
  3.8 1.0 %copy-done.3 = bf16[256,1024]{1,0:T(8,128)(2,1)S(1)} copy-done((bf16[256,1024]{1,0:T(8,128)(2,1)S(1)}, bf16[256,1024]{1,0:T(8,128)(2,1)}, u32[]{:S(2)}) %copy-start.3) | copy-done | bytes 524312
  4.8 0.0 copy-start.4
  4.8 0.7 %copy-done.4 = f32[8,256]{1,0:T(8,128)S(1)} copy-done((f32[8,256]{1,0:T(8,128)S(1)}, f32[8,256]{1,0:T(8,128)}, u32[]{:S(2)}) %copy-start.4) | copy-done | bytes 8216
  5.5 60.0 %shard_map.84 = (bf16[256,1024]{1,0:T(8,128)(2,1)S(1)}, bf16[256,1024]{1,0:T(8,128)(2,1)S(1)}, bf16[256,1024]{1,0:T(8,128)(2,1)S(1)}, bf16[256,1024]{1,0:T(8,128)(2,1)S(1)}) custom-call(bf16[256,1024]{1,0:T(8,128)(2,1)S(1)} %copy-done, bf16[256,1024]{1,0:T(8,128)(2,1)S(1)} %copy-done.1, bf16[256,1024]{1,0:T(8,128)(2,1)S(1)} %copy-done.2, ...), custom_call_target="tpu_custom_call" | custom-call | tf_op jit(solution)/shard_map/pallas_call | solution.py:198
  65.6 0.8 %copy.13 = bf16[256,1024]{1,0:T(8,128)(2,1)} copy(bf16[256,1024]{1,0:T(8,128)(2,1)S(1)} %get-tuple-element.8) | data formatting | bytes 1048576
  66.3 0.8 %copy.14 = bf16[256,1024]{1,0:T(8,128)(2,1)} copy(bf16[256,1024]{1,0:T(8,128)(2,1)S(1)} %get-tuple-element.9) | data formatting | bytes 1048576
  67.1 0.8 %copy.15 = bf16[256,1024]{1,0:T(8,128)(2,1)} copy(bf16[256,1024]{1,0:T(8,128)(2,1)S(1)} %get-tuple-element.10) | data formatting | bytes 1048576
  67.9 0.8 %copy.16 = bf16[256,1024]{1,0:T(8,128)(2,1)} copy(bf16[256,1024]{1,0:T(8,128)(2,1)S(1)} %get-tuple-element.11) | data formatting | bytes 1048576
Async XLA Ops:
  0.6 1.0 %copy-start = (bf16[256,1024]{1,0:T(8,128)(2,1)S(1)}, bf16[256,1024]{1,0:T(8,128)(2,1)}, u32[]{:S(2)}) copy-start(bf16[256,1024]{1,0:T(8,128)(2,1)} %q_ref.1) | copy-start | bytes 1572868
  1.7 1.0 %copy-start.1 = (bf16[256,1024]{1,0:T(8,128)(2,1)S(1)}, bf16[256,1024]{1,0:T(8,128)(2,1)}, u32[]{:S(2)}) copy-start(bf16[256,1024]{1,0:T(8,128)(2,1)} %k_ref.1) | copy-start | bytes 1572868
  2.7 1.0 %copy-start.2 = (bf16[256,1024]{1,0:T(8,128)(2,1)S(1)}, bf16[256,1024]{1,0:T(8,128)(2,1)}, u32[]{:S(2)}) copy-start(bf16[256,1024]{1,0:T(8,128)(2,1)} %v_ref.1) | copy-start | bytes 1572868
  3.8 1.0 %copy-start.3 = (bf16[256,1024]{1,0:T(8,128)(2,1)S(1)}, bf16[256,1024]{1,0:T(8,128)(2,1)}, u32[]{:S(2)}) copy-start(bf16[256,1024]{1,0:T(8,128)(2,1)} %g_ref.1) | copy-start | bytes 1572868
  4.8 0.7 %copy-start.4 = (f32[8,256]{1,0:T(8,128)S(1)}, f32[8,256]{1,0:T(8,128)}, u32[]{:S(2)}) copy-start(f32[8,256]{1,0:T(8,128)} %decay_ref.1) | copy-start | bytes 24580

commit v2 on v1

v2 whole, which is shorter than its diff:
```python
import functools
import math

import jax
import jax.numpy as jnp
from jax import lax
from jax.experimental import pallas as pl
from jax.experimental.pallas import tpu as pltpu
from jax.sharding import PartitionSpec as P

EPSILON = 1e-06
F32 = jnp.float32
BF16 = jnp.bfloat16
MESH = pl.DeviceIdType.MESH
PARTS = 2


def dot(a, b, da, db):
    return lax.dot_general(a, b, (((da,), (db,)), ((), ())), preferred_element_type=F32)


def kernel(outer_size, inner_size, parts, q_hbm, k_hbm, v_hbm, decay_hbm, g_hbm,
           att_ref, gq_ref, gk_ref, gv_ref,
           q_ref, k_ref, v_ref, decay_ref, g_ref,
           run_ref, col_ref, tot_ref, fac_ref, facs_ref, dec_ref, w_ref, kd_ref, mix_ref, gm_ref,
           send1, recv1, out1, ret1, agg1, send2, recv2, out2, ret2, agg2, ent_ref, gkl_ref, gvl_ref,
           load_sems, fac_sems, send_sems, recv_sems):
    n = outer_size * inner_size
    half_inner = inner_size // 2
    count = n // 2
    heads, tokens = decay_ref.shape
    size = q_ref.shape[1] // heads
    scaling = 1.0 / math.sqrt(size)
    per_head = count // heads
    rows = size // (per_head * parts)
    place_o, place_i = lax.axis_index("outer"), lax.axis_index("inner")
    half = place_i // half_inner
    me = place_o * inner_size + place_i
    seat = place_o * half_inner + place_i % half_inner

    loads = [pltpu.make_async_copy(source, target, load_sems.at[at]) for at, (source, target) in enumerate(
        ((decay_hbm, decay_ref), (k_hbm, k_ref), (v_hbm, v_ref), (q_hbm, q_ref), (g_hbm, g_ref)))]
    for load in loads:
        load.start()

    def everyone(act):
        def turn(i, carry):
            at = (me + 1 + i) % n
            act(at // inner_size, at % inner_size)
            return carry
        lax.fori_loop(0, n - 1, turn, 0)

    def seat_of(o, i):
        return o * half_inner + i % half_inner

    barrier = pltpu.get_barrier_semaphore()
    everyone(lambda o, i: pl.semaphore_signal(barrier, inc=1, device_id=(o, i), device_id_type=MESH))

    def exchange(source, target, phase, part):
        def turn(i, carry):
            step = i + 1
            o = (place_o + step % outer_size) % outer_size
            i = half * half_inner + (place_i % half_inner + step // outer_size) % half_inner
            pltpu.make_async_remote_copy(
                src_ref=source.at[part, seat_of(o, i)], dst_ref=target.at[part, seat],
                send_sem=send_sems.at[phase, part], recv_sem=recv_sems.at[phase, part],
                device_id=(o, i), device_id_type=MESH).start()
            return carry
        lax.fori_loop(0, count - 1, turn, 0)

    def across(sums, phase, part):
        pltpu.make_async_remote_copy(
            src_ref=sums.at[part, half], dst_ref=sums.at[part, half],
            send_sem=send_sems.at[phase, part], recv_sem=recv_sems.at[phase, part],
            device_id=(place_o, (place_i + half_inner) % inner_size), device_id_type=MESH).start()

    def drain(piece, sem):
        pltpu.make_async_copy(piece, piece, sem).wait()

    def others(buffer, part):
        return buffer.at[part, pl.ds(0, count - 1)]

    def each_head(act):
        def turn(i, carry):
            act(2 * i)
            act(2 * i + 1)
            return carry
        lax.fori_loop(0, heads // 2, turn, 0)

    def span(h):
        return pl.ds(pl.multiple_of(h * size, size), size)

    def put_state(target, h, state):
        for p in range(per_head):
            for part in range(parts):
                first = (p * parts + part) * rows
                target[part, h * per_head + p] = state[first:first + rows]

    def get_state(source, h):
        return jnp.concatenate(
            [source[part, h * per_head + p] for p in range(per_head) for part in range(parts)], axis=0)

    loads[0].wait()
    running = decay_ref[...]
    lane = lax.broadcasted_iota(jnp.int32, (heads, tokens), 1)
    shift = 1
    while shift < tokens:
        running = running + jnp.where(lane >= shift, pltpu.roll(running, shift, 1), 0.0)
        shift *= 2
    run_ref[...] = running
    for h in range(heads):
        row = running[h:h + 1]
        col_ref[h] = jnp.broadcast_to(row, (size, tokens)).T
        total = jnp.broadcast_to(row[:, tokens - 1:], (1, size))
        tot_ref[h] = total
        fac_ref[h] = jnp.exp(total)
    loads[1].wait()
    loads[2].wait()

    def state_of(h):
        cols = span(h)
        shrink = jnp.exp(tot_ref[h] - col_ref[h])
        key_dec = (k_ref[:, cols].astype(F32) * shrink).astype(BF16)
        kd_ref[:, cols] = key_dec
        put_state(send1, h, dot(key_dec, v_ref[:, cols], 0, 0))

    each_head(state_of)
    pl.semaphore_wait(barrier, n - 1)

    def send_factor(o, i):
        pltpu.make_async_remote_copy(
            src_ref=fac_ref.at[seat_of(o, i) // per_head], dst_ref=facs_ref.at[me],
            send_sem=fac_sems.at[0], recv_sem=fac_sems.at[1],
            device_id=(o, i), device_id_type=MESH).start()

    exchange(send1, recv1, 0, 0)
    everyone(send_factor)
    for part in range(1, parts):
        exchange(send1, recv1, 0, part)
    facs_ref[me] = fac_ref[seat // per_head]
    for part in range(parts):
        recv1[part, seat] = send1[part, seat]

    t_index = lax.broadcasted_iota(jnp.int32, (tokens, tokens), 0)
    s_index = lax.broadcasted_iota(jnp.int32, (tokens, tokens), 1)
    causal = s_index <= t_index

    def local_mix(h):
        cols = span(h)
        column = jnp.concatenate([col_ref[h]] * (tokens // size), axis=1)
        gaps = column - run_ref[pl.ds(h, 1)]
        decay = jnp.where(causal, jnp.exp(jnp.where(causal, gaps, 0.0)), 0.0) * scaling
        dec_ref[h] = decay
        weights = (dot(q_ref[:, cols], k_ref[:, cols], 1, 1) * decay).astype(BF16)
        w_ref[h] = weights
        mix_ref[:, cols] = dot(weights, v_ref[:, cols], 1, 0)

    def group_sums(source, sums, part, backward):
        def group(o, carry):
            state = jnp.zeros((rows, size), F32)
            for step in range(half_inner):
                at = half_inner - 1 - step if backward else step
                factor = facs_ref[o * inner_size + half * half_inner + at]
                state = factor * state + source[part, o * half_inner + at]
            sums[part, half, o] = state
            return carry
        lax.fori_loop(0, outer_size, group, 0)

    def scan(source, sums, target, part, backward):
        order = (1, 0) if backward else (0, 1)

        def group(turn, carry):
            o = outer_size - 1 - turn if backward else turn
            entry = []
            for side in order:
                entry.append(carry)
                factor = facs_ref[o * inner_size + side * half_inner]
                for step in range(1, half_inner):
                    factor = factor * facs_ref[o * inner_size + side * half_inner + step]
                carry = factor * carry + sums[part, side, o]
            state = jnp.where(half == order[0], entry[0], entry[1])
            for step in range(half_inner):
                at = half_inner - 1 - step if backward else step
                target[part, o * half_inner + at] = state
                factor = facs_ref[o * inner_size + half * half_inner + at]
                state = factor * state + source[part, o * half_inner + at]
            return carry
        lax.fori_loop(0, outer_size, group, jnp.zeros((rows, size), F32))

    def carried(source, sums, target, result, phase, backward):
        for part in range(parts):
            drain(others(source, part), recv_sems.at[phase, part])
            group_sums(source, sums, part, backward)
            across(sums, phase + 1, part)
        for part in range(parts):
            drain(sums.at[part, 1 - half], recv_sems.at[phase + 1, part])
            scan(source, sums, target, part, backward)
            exchange(target, result, phase + 2, part)
            result[part, seat] = target[part, seat]

    loads[3].wait()
    drain(facs_ref.at[pl.ds(0, n - 1)], fac_sems.at[1])
    each_head(local_mix)
    carried(recv1, agg1, out1, ret1, 0, False)
    loads[4].wait()
    for part in range(parts):
        drain(others(ret1, part), recv_sems.at[2, part])

    def mix(h):
        cols = span(h)
        entering = get_state(ret1, h).astype(BF16)
        ent_ref[h] = entering
        growth = jnp.exp(col_ref[h])
        query_dec = (q_ref[:, cols].astype(F32) * growth).astype(BF16)
        mixed = mix_ref[:, cols] + scaling * dot(query_dec, entering, 1, 0)
        inverse = lax.rsqrt(jnp.mean(mixed * mixed, axis=1, keepdims=True) + EPSILON)
        normed = mixed * inverse
        att_ref[:, cols] = normed.astype(BF16)
        g = g_ref[:, cols].astype(F32)
        grad_mixed = (inverse * (g - normed * jnp.mean(g * normed, axis=1, keepdims=True))).astype(BF16)
        gm_ref[:, cols] = grad_mixed
        put_state(send2, h, scaling * dot(query_dec, grad_mixed, 0, 0))

    each_head(mix)
    for part in range(parts):
        exchange(send2, recv2, 3, part)
    for part in range(parts):
        recv2[part, seat] = send2[part, seat]

    def local_grads(h):
        cols = span(h)
        grad_mixed = gm_ref[:, cols]
        grad_score = (dot(grad_mixed, v_ref[:, cols], 1, 1) * dec_ref[h]).astype(BF16)
        far = (scaling * jnp.exp(col_ref[h])) * dot(grad_mixed, ent_ref[h], 1, 1)
        gq_ref[:, cols] = (dot(grad_score, k_ref[:, cols], 1, 0) + far).astype(BF16)
        gkl_ref[:, cols] = dot(grad_score, q_ref[:, cols], 0, 0)
        gvl_ref[:, cols] = dot(w_ref[h], grad_mixed, 0, 0)

    each_head(local_grads)
    carried(recv2, agg2, out2, ret2, 3, True)
    for part in range(parts):
        drain(others(ret2, part), recv_sems.at[5, part])

    def far_grads(h):
        cols = span(h)
        leaving = get_state(ret2, h).astype(BF16)
        shrink = jnp.exp(tot_ref[h] - col_ref[h])
        gk_ref[:, cols] = (gkl_ref[:, cols] + shrink * dot(v_ref[:, cols], leaving, 1, 1)).astype(BF16)
        gv_ref[:, cols] = (gvl_ref[:, cols] + dot(kd_ref[:, cols], leaving, 1, 0)).astype(BF16)

    each_head(far_grads)
    drain(facs_ref.at[pl.ds(0, n - 1)], fac_sems.at[0])
    for part in range(parts):
        for phase, buffer in ((0, send1), (2, out1), (3, send2), (5, out2)):
            drain(others(buffer, part), send_sems.at[phase, part])
        drain(agg1.at[part, half], send_sems.at[1, part])
        drain(agg2.at[part, half], send_sems.at[4, part])


def store(*refs):
    sources, targets, sems = refs[:4], refs[4:8], refs[8]
    copies = [pltpu.make_async_copy(s, t, sems.at[at]) for at, (s, t) in enumerate(zip(sources, targets))]
    for copy in copies:
        copy.start()
    for copy in copies:
        copy.wait()


def body(outer_size, inner_size, query_rows, key_rows, value_rows, log_decay, grad_out):
    n = outer_size * inner_size
    heads, tokens = log_decay.shape
    wide = query_rows.shape[1]
    size = wide // heads
    count = n // 2
    chunk = heads * size // count
    parts = PARTS if chunk % (8 * PARTS) == 0 else 1
    rows = chunk // parts
    pieces = pltpu.VMEM((parts, count, rows, size), F32)
    sums = pltpu.VMEM((parts, 2, outer_size, rows, size), F32)
    vmem = pl.BlockSpec(memory_space=pltpu.VMEM)
    hbm = pl.BlockSpec(memory_space=pltpu.HBM)
    row_block = pltpu.VMEM((tokens, wide), BF16)
    outs = [jax.ShapeDtypeStruct((tokens, wide), BF16)] * 4
    results = pl.pallas_call(
        functools.partial(kernel, outer_size, inner_size, parts),
        out_shape=outs,
        in_specs=[hbm] * 5,
        out_specs=[vmem] * 4,
        scratch_shapes=[
            row_block, row_block, row_block, pltpu.VMEM((heads, tokens), F32), row_block,
            pltpu.VMEM((heads, tokens), F32),
            pltpu.VMEM((heads, tokens, size), F32),
            pltpu.VMEM((heads, 1, size), F32),
            pltpu.VMEM((heads, 1, size), F32),
            pltpu.VMEM((n, 1, size), F32),
            pltpu.VMEM((heads, tokens, tokens), F32),
            pltpu.VMEM((heads, tokens, tokens), BF16),
            row_block,
            pltpu.VMEM((tokens, wide), F32),
            row_block,
            pieces, pieces, pieces, pieces, sums, pieces, pieces, pieces, pieces, sums,
            pltpu.VMEM((heads, size, size), BF16),
            pltpu.VMEM((tokens, wide), F32),
            pltpu.VMEM((tokens, wide), F32),
            pltpu.SemaphoreType.DMA((5,)),
            pltpu.SemaphoreType.DMA((2,)),
            pltpu.SemaphoreType.DMA((6, parts)),
            pltpu.SemaphoreType.DMA((6, parts)),
        ],
        compiler_params=pltpu.CompilerParams(
            collective_id=0, has_side_effects=True, vmem_limit_bytes=40 * 1024 * 1024),
    )(query_rows, key_rows, value_rows, log_decay, grad_out)
    return pl.pallas_call(
        store,
        out_shape=outs,
        in_specs=[vmem] * 4,
        out_specs=[hbm] * 4,
        scratch_shapes=[pltpu.SemaphoreType.DMA((4,))],
        compiler_params=pltpu.CompilerParams(vmem_limit_bytes=8 * 1024 * 1024),
    )(*results)


def solution(mesh):
    both = ("outer", "inner")
    row_spec = P(both, None)
    return jax.shard_map(
        functools.partial(body, mesh.shape["outer"], mesh.shape["inner"]),
        mesh=mesh,
        in_specs=(row_spec, row_spec, row_spec, P(None, both), row_spec),
        out_specs=(row_spec,) * 4,
        check_vma=False,
    )
```

time: 69.1 us -> 60.1 us (0.87)
  Pallas kernels: 60 us -> 54.3 us
  local copies, waits for them, and re-layouts: 8.03 us -> 4.85 us
    pallas_call x1 -> x2, Pallas kernels: 60 us -> 54.3 us  [the longest x1 52.9 us: body(): pl.pallas_call(functools.partial(kernel, outer_size, inner_size, parts),...]
    unnamed x14 -> x10, local copies, waits for them, and re-layouts: 8.03 us -> 4.85 us
where the time goes in v2:
time: 60.1 us; the launch traced here: 59.8 us
  Pallas kernels  54.3 us (90%)
  local copies, waits for them, and re-layouts  4.85 us (8%)
  between operations  0.65 us (1%)
    pallas_call x1, Pallas kernels, body(): pl.pallas_call(functools.partial(kernel, outer_size, inner_size, parts),...  52.9 us
    unnamed x10, local copies, waits for them, and re-layouts  4.85 us
    pallas_call x1, Pallas kernels, body(): pl.pallas_call(store, out_shape=outs, in_specs=[vmem] * 4, out_specs=[hbm...  1.35 us

profile of v2, /device:TPU:0, one launch (start us, length us, event | category | flops | bytes accessed | tf_op | source)
XLA Modules:
  0.0 59.8 jit_solution(16180384554536018531)
XLA Ops:
  0.6 0.0 copy-start
  0.6 1.0 %copy-done = bf16[256,1024]{1,0:T(8,128)(2,1)S(1)} copy-done((bf16[256,1024]{1,0:T(8,128)(2,1)S(1)}, bf16[256,1024]{1,0:T(8,128)(2,1)}, u32[]{:S(2)}) %copy-start) | copy-done | bytes 524312
  1.7 0.0 copy-start.1
  1.7 1.0 %copy-done.1 = bf16[256,1024]{1,0:T(8,128)(2,1)S(1)} copy-done((bf16[256,1024]{1,0:T(8,128)(2,1)S(1)}, bf16[256,1024]{1,0:T(8,128)(2,1)}, u32[]{:S(2)}) %copy-start.1) | copy-done | bytes 524312
  2.7 0.0 copy-start.2
  2.7 1.0 %copy-done.2 = bf16[256,1024]{1,0:T(8,128)(2,1)S(1)} copy-done((bf16[256,1024]{1,0:T(8,128)(2,1)S(1)}, bf16[256,1024]{1,0:T(8,128)(2,1)}, u32[]{:S(2)}) %copy-start.2) | copy-done | bytes 524312
  3.8 0.0 copy-start.3
  3.8 1.0 %copy-done.3 = bf16[256,1024]{1,0:T(8,128)(2,1)S(1)} copy-done((bf16[256,1024]{1,0:T(8,128)(2,1)S(1)}, bf16[256,1024]{1,0:T(8,128)(2,1)}, u32[]{:S(2)}) %copy-start.3) | copy-done | bytes 524312
  4.8 0.0 copy-start.4
  4.8 0.7 %copy-done.4 = f32[8,256]{1,0:T(8,128)S(1)} copy-done((f32[8,256]{1,0:T(8,128)S(1)}, f32[8,256]{1,0:T(8,128)}, u32[]{:S(2)}) %copy-start.4) | copy-done | bytes 8216
  5.5 52.9 %shard_map.84 = (bf16[256,1024]{1,0:T(8,128)(2,1)S(1)}, bf16[256,1024]{1,0:T(8,128)(2,1)S(1)}, bf16[256,1024]{1,0:T(8,128)(2,1)S(1)}, bf16[256,1024]{1,0:T(8,128)(2,1)S(1)}) custom-call(bf16[256,1024]{1,0:T(8,128)(2,1)S(1)} %copy-done, bf16[256,1024]{1,0:T(8,128)(2,1)S(1)} %copy-done.1, bf16[256,1024]{1,0:T(8,128)(2,1)S(1)} %copy-done.2, ...), custom_call_target="tpu_custom_call" | custom-call | tf_op jit(solution)/shard_map/pallas_call | solution.py:284
  58.5 1.3 %shard_map.85 = (bf16[256,1024]{1,0:T(8,128)(2,1)}, bf16[256,1024]{1,0:T(8,128)(2,1)}, bf16[256,1024]{1,0:T(8,128)(2,1)}, bf16[256,1024]{1,0:T(8,128)(2,1)}) custom-call(bf16[256,1024]{1,0:T(8,128)(2,1)S(1)} %get-tuple-element.8.refs_0_, bf16[256,1024]{1,0:T(8,128)(2,1)S(1)} %get-tuple-element.9.refs_1_, bf16[256,1024]{1,0:T(8,128)(2,1)S(1)} %get-tuple-element.10.refs_2_, ...), custom_call_target="tpu_custom_call" | custom-call | tf_op jit(solution)/shard_map/pallas_call | solution.py:313
Async XLA Ops:
  0.6 1.0 %copy-start = (bf16[256,1024]{1,0:T(8,128)(2,1)S(1)}, bf16[256,1024]{1,0:T(8,128)(2,1)}, u32[]{:S(2)}) copy-start(bf16[256,1024]{1,0:T(8,128)(2,1)} %q_hbm.1) | copy-start | bytes 1572868
  1.7 1.0 %copy-start.1 = (bf16[256,1024]{1,0:T(8,128)(2,1)S(1)}, bf16[256,1024]{1,0:T(8,128)(2,1)}, u32[]{:S(2)}) copy-start(bf16[256,1024]{1,0:T(8,128)(2,1)} %k_hbm.1) | copy-start | bytes 1572868
  2.7 1.0 %copy-start.2 = (bf16[256,1024]{1,0:T(8,128)(2,1)S(1)}, bf16[256,1024]{1,0:T(8,128)(2,1)}, u32[]{:S(2)}) copy-start(bf16[256,1024]{1,0:T(8,128)(2,1)} %v_hbm.1) | copy-start | bytes 1572868
  3.8 1.0 %copy-start.3 = (bf16[256,1024]{1,0:T(8,128)(2,1)S(1)}, bf16[256,1024]{1,0:T(8,128)(2,1)}, u32[]{:S(2)}) copy-start(bf16[256,1024]{1,0:T(8,128)(2,1)} %g_hbm.1) | copy-start | bytes 1572868
  4.8 0.7 %copy-start.4 = (f32[8,256]{1,0:T(8,128)S(1)}, f32[8,256]{1,0:T(8,128)}, u32[]{:S(2)}) copy-start(f32[8,256]{1,0:T(8,128)} %decay_hbm.1) | copy-start | bytes 24580

commit v3 on v2

--- a/solution.py
+++ b/solution.py
@@ -12,7 +12,7 @@
 F32 = jnp.float32
 BF16 = jnp.bfloat16
 MESH = pl.DeviceIdType.MESH
-PARTS = 2
+PARTS = 4
 
 
 def dot(a, b, da, db):
@@ -309,7 +309,7 @@
         ],
         compiler_params=pltpu.CompilerParams(
             collective_id=0, has_side_effects=True, vmem_limit_bytes=40 * 1024 * 1024),
-    )(query_rows, key_rows, value_rows, log_decay, grad_out)
+    )(*[pltpu.with_memory_space_constraint(x, pltpu.HBM) for x in (query_rows, key_rows, value_rows, log_decay, grad_out)])
     return pl.pallas_call(
         store,
         out_shape=outs,

time: 60.1 us -> 51.8 us (0.86)
  local copies, waits for them, and re-layouts: 4.85 us -> 0 us
  Pallas kernels: 54.3 us -> 51 us
    unnamed x10 -> x0, local copies, waits for them, and re-layouts: 4.85 us -> none
    pallas_call x1, Pallas kernels: 52.9 us -> 49.6 us  [body(): pl.pallas_call(functools.partial(kernel, outer_size, inner_size, parts),...]
where the time goes in v3:
time: 51.8 us; the launch traced here: 51.6 us
  Pallas kernels  51 us (98%)
  between operations  0.64 us (1%)
    pallas_call x1, Pallas kernels, body(): pl.pallas_call(functools.partial(kernel, outer_size, inner_size, parts),...  49.6 us
    pallas_call x1, Pallas kernels, body(): pl.pallas_call(store, out_shape=outs, in_specs=[vmem] * 4, out_specs=[hbm...  1.35 us

profile of v3, /device:TPU:0, one launch (start us, length us, event | category | flops | bytes accessed | tf_op | source)
XLA Modules:
  0.0 51.6 jit_solution(3038178433001219170)
XLA Ops:
  0.6 49.6 %shard_map.84 = (bf16[256,1024]{1,0:T(8,128)(2,1)S(1)}, bf16[256,1024]{1,0:T(8,128)(2,1)S(1)}, bf16[256,1024]{1,0:T(8,128)(2,1)S(1)}, bf16[256,1024]{1,0:T(8,128)(2,1)S(1)}) custom-call(bf16[256,1024]{1,0:T(8,128)(2,1)} %q_hbm.1, bf16[256,1024]{1,0:T(8,128)(2,1)} %k_hbm.1, bf16[256,1024]{1,0:T(8,128)(2,1)} %v_hbm.1, f32[8,256]{1,0:T(8,128)} %decay_hbm.1, ...), custom_call_target="tpu_custom_call" | custom-call | tf_op jit(solution)/shard_map/pallas_call | solution.py:284
  50.3 1.3 %shard_map.85 = (bf16[256,1024]{1,0:T(8,128)(2,1)}, bf16[256,1024]{1,0:T(8,128)(2,1)}, bf16[256,1024]{1,0:T(8,128)(2,1)}, bf16[256,1024]{1,0:T(8,128)(2,1)}) custom-call(bf16[256,1024]{1,0:T(8,128)(2,1)S(1)} %get-tuple-element.8.refs_0_, bf16[256,1024]{1,0:T(8,128)(2,1)S(1)} %get-tuple-element.9.refs_1_, bf16[256,1024]{1,0:T(8,128)(2,1)S(1)} %get-tuple-element.10.refs_2_, ...), custom_call_target="tpu_custom_call" | custom-call | tf_op jit(solution)/shard_map/pallas_call | solution.py:313
